TPU v7x, 256 devices: a 4x2x16 block of a 4x16x16 slice. The times are simulated.
256 devices in a mesh: group: 2 (over y), seq: 128 (over x, z, core).
Axes of the slice: x: 4, y: 2, z: 16, core: 2. Of those that a mesh axis runs over, the one named last changes fastest.
The devices are a block of a 4x16x16 slice.
Arguments:
- query_frames: bfloat16 [131072, 4096], P(('group', 'seq')), parts along dimension 0, may hold values from -5 to 5
- key_frames: bfloat16 [131072, 512], P(('group', 'seq')), parts along dimension 0, may hold values from -5 to 5
- value_frames: bfloat16 [131072, 512], P(('group', 'seq')), parts along dimension 0, may hold values from -6 to 6
- token_counts: int32 [256], P(('group', 'seq')), parts along dimension 0, may hold values from 1 to 511, as said below
- segments: int32 [65536], P('group'), parts along dimension 0, may hold values from 0 to 63, as said below
Outputs:
- attended: bfloat16 [65536, 4096], P(('group', 'seq')), parts along dimension 0
There are 2 independent parts, one for each index of `group`. A program takes and returns all parts, laid end to end along the dimension named above; each array names one. Nothing has to cross between parts.
Inputs may be any that keep to these rules, and one draw needn't show every extreme that they name: `token_counts`: entry d belongs to device d of seq. The counts before entry d sum to a number from d * 256 to d * 256 + 255, and all counts sum to 32768. `segments`: sequence numbers never fall along the positions and each of 0 to 63 appears; each packed sequence covers 1 to 1024 consecutive positions, one exactly 1024; the first covers more than 256.
All inputs are finite; a program needn't handle non-finite values.
Results may differ from a plain program's by a relative error of at most 0.013.
Values may be sent and summed in bfloat16 or wider, within the bound.
A program may use at most 64 MiB of HBM per device.

v0:
```python
import math

import jax
import jax.numpy as jnp
from jax import lax
from jax.sharding import Mesh
from jax.sharding import PartitionSpec as P

Q_HEADS = 32
KV_HEADS = 4
HEAD_DIM = 128
SPAN = 256
WINDOW = 5
SEQ = ("seq_0", "seq_1", "seq_2")
GROUP_SEQ = ("group", "seq_0", "seq_1", "seq_2")


def in_order(tiles, dim):
    tiles = jnp.moveaxis(tiles, 0, dim)
    lengths = tiles.shape
    return tiles.reshape(*lengths[:dim], lengths[dim] * lengths[dim + 1], *lengths[dim + 2 :])


def gather_in_order(x, axes, order):
    tiles = x[None]
    for k in order:
        tiles = lax.all_gather(tiles, axes[k], axis=0, tiled=True)
    carried = [lax.axis_size(axes[k]) for k in reversed(order)]
    tiles = tiles.reshape(*carried, *x.shape)
    turned = sorted(range(len(order)), key=lambda place: order[len(order) - 1 - place])
    return tiles.transpose(*turned, *range(len(order), tiles.ndim)).reshape(-1, *x.shape)


def gathered_by_axis(x, axes, order, dim):
    return in_order(gather_in_order(x, axes, order), dim)


def passed_along(block, axis, distance):
    devices = range(lax.axis_size(axis))
    route = [(i - distance, i) for i in devices if i - distance in devices]
    return lax.ppermute(block, axis, route)


def attend_block(running, query_rows, key_rows, value_rows, query_part, key_part, segments):
    groups = Q_HEADS // KV_HEADS
    positions = jnp.arange(SPAN, dtype=jnp.int32)
    query_place = query_part * SPAN + positions
    key_place = key_part * SPAN + positions
    query_clip = lax.dynamic_slice_in_dim(segments, query_part * SPAN, SPAN, 0)
    key_clip = lax.dynamic_slice_in_dim(segments, key_part * SPAN, SPAN, 0)
    allowed = (key_place[None, :] <= query_place[:, None]) & (
        key_clip[None, :] == query_clip[:, None]
    )
    highest, totals, summed = running
    scores = jnp.einsum(
        "qhgd,khd->hgqk",
        query_rows.reshape(SPAN, KV_HEADS, groups, HEAD_DIM),
        key_rows.reshape(SPAN, KV_HEADS, HEAD_DIM),
        preferred_element_type=jnp.float32,
    ) * (1.0 / math.sqrt(HEAD_DIM))
    scores = jnp.where(allowed, scores, -jnp.inf)
    new_highest = jnp.maximum(highest, jnp.max(scores, axis=-1))
    factor = jnp.exp(highest - new_highest)
    weights = jnp.exp(scores - new_highest[..., None])
    totals = totals * factor + jnp.sum(weights, axis=-1)
    product = jnp.einsum(
        "hgqk,khd->qhgd",
        weights.astype(jnp.bfloat16),
        value_rows.reshape(SPAN, KV_HEADS, HEAD_DIM),
        preferred_element_type=jnp.float32,
    )
    factor_rows = jnp.transpose(factor, (2, 0, 1))[..., None]
    summed = (summed.reshape(SPAN, KV_HEADS, groups, HEAD_DIM) * factor_rows + product).reshape(
        SPAN, Q_HEADS * HEAD_DIM
    )
    return (new_highest, totals, summed)


def finish(running):
    highest, totals, summed = running
    divisor = jnp.transpose(totals, (2, 0, 1)).reshape(SPAN, Q_HEADS, 1)
    return (
        (summed.reshape(SPAN, Q_HEADS, HEAD_DIM) / divisor)
        .reshape(SPAN, Q_HEADS * HEAD_DIM)
        .astype(jnp.bfloat16)
    )


def shards(query_frames, key_frames, value_frames, token_counts, segments):
    seq_count = lax.axis_size(SEQ)
    device = lax.axis_index(SEQ)
    every_count = gathered_by_axis(token_counts, (("seq_0", "seq_1"), "seq_2"), (0, 1), 0)
    before = jnp.sum(jnp.where(jnp.arange(seq_count, dtype=jnp.int32) < device, every_count, 0))
    lead_in = before - device * SPAN
    lead_out = lead_in + token_counts[0] - SPAN
    positions = jnp.arange(SPAN, dtype=jnp.int32)[:, None]

    def own_rows(frames):
        padded = jnp.concatenate([jnp.zeros((SPAN, frames.shape[1]), frames.dtype), frames], axis=0)
        return lax.dynamic_slice_in_dim(padded, SPAN - lead_in, SPAN, 0)

    def tail_rows(frames):
        sliced = lax.dynamic_slice_in_dim(frames, SPAN - lead_in, SPAN, 0)
        return jnp.where(positions < lead_out, sliced, jnp.zeros_like(sliced))

    arrived = passed_along(
        (tail_rows(query_frames), tail_rows(key_frames), tail_rows(value_frames)), SEQ, 1
    )
    early = positions < lead_in
    queries = jnp.where(early, arrived[0], own_rows(query_frames))
    key_rows = jnp.where(early, arrived[1], own_rows(key_frames))
    value_rows = jnp.where(early, arrived[2], own_rows(value_frames))
    groups = Q_HEADS // KV_HEADS
    initial = (
        jnp.full((KV_HEADS, groups, SPAN), -1e30, jnp.float32),
        jnp.zeros((KV_HEADS, groups, SPAN), jnp.float32),
        jnp.zeros((SPAN, Q_HEADS * HEAD_DIM), jnp.float32),
    )
    running = attend_block(initial, queries, key_rows, value_rows, device, device, segments)

    def visit(turn_number, carried):
        moving, current = carried
        moving = passed_along((moving[0], moving[1]), SEQ, 1)
        block_number = (device - turn_number) % seq_count
        return (
            moving,
            attend_block(current, queries, moving[0], moving[1], device, block_number, segments),
        )

    carried = lax.fori_loop(1, WINDOW, visit, ((key_rows, value_rows), running))
    return finish(carried[1])


def solution(mesh):
    split = Mesh(
        mesh.devices.reshape(mesh.shape["group"], 4, 16, 2), ("group", "seq_0", "seq_1", "seq_2")
    )
    return jax.shard_map(
        shards,
        mesh=split,
        in_specs=(
            P(GROUP_SEQ, None),
            P(GROUP_SEQ, None),
            P(GROUP_SEQ, None),
            P(GROUP_SEQ),
            P("group"),
        ),
        out_specs=P(GROUP_SEQ, None),
        check_vma=False,
    )
```

profile of v0, /device:TPU:46, one launch (start us, length us, event | category | flops | bytes accessed | tf_op | source)
XLA Modules:
  0.0 190.7 jit_solution(6104175651337297565)
XLA Ops:
  2.6 43.5 %all-reduce.3 = s32[64]{0:T(128)S(1)} all-reduce(s32[64]{0:T(128)S(1)} %dynamic-update-slice), channel_id=2, replica_groups=mesh['group'=2,'seq_0'=4,'seq_1'=16,'seq_2'=2] {'seq_0','seq_1'}, use_global_device_ids=true, to_apply=%add.3 | all-reduce | flops 64 | bytes 512
  48.2 1.8 all-reduce.4
  51.4 2.4 %dynamic-slice_select_fusion = bf16[256,4096]{1,0:T(8,128)(2,1)S(1)} fusion(bf16[512,4096]{1,0:T(8,128)(2,1)} %param.7, s32[]{:T(128)S(6)} %select_n.91, pred[256]{0:T(512)(128)(4,1)S(1)} %iota_compare_fusion), kind=kLoop, calls=%fused_computation.38 | loop fusion | flops 1048576 | bytes 4194564 | tf_op jit(solution)/shard_map/jit(_where)/select_n | solution.py:104
  53.7 2.1 %collective-permute-start.4 = (bf16[256,4096]{1,0:T(8,128)(2,1)S(1)}, bf16[256,4096]{1,0:T(8,128)(2,1)}, u32[]{:S(2)}, u32[]{:S(2)}) collective-permute-start(bf16[256,4096]{1,0:T(8,128)(2,1)S(1)} %dynamic-slice_select_fusion), channel_id=1, source_target_pairs={{0,1},{1,2},{2,3},{3,4},{4,5},{5,6},{6,7},{7,8},{8,9},{9,10},{10,1... | collective-permute-start | bytes 6291464 | tf_op jit(solution)/shard_map/ppermute | solution.py:41
  58.3 3.8 %collective-permute-start.2 = (bf16[256,512]{0,1:T(8,128)(2,1)}, bf16[256,512]{0,1:T(8,128)(2,1)}, u32[]{:S(2)}, u32[]{:S(2)}) collective-permute-start(bf16[256,512]{0,1:T(8,128)(2,1)} %get-tuple-element.288), channel_id=1, source_target_pairs={{0,1},{1,2},{2,3},{3,4},{4,5},{5,6},{6,7},{7,8},{8,9},{9,10},{10,1... | collective-permute-start | bytes 786440 | tf_op jit(solution)/shard_map/ppermute | solution.py:41
  62.0 2.1 %collective-permute-start.3 = (bf16[256,512]{0,1:T(8,128)(2,1)S(1)}, bf16[256,512]{0,1:T(8,128)(2,1)}, u32[]{:S(2)}, u32[]{:S(2)}) collective-permute-start(bf16[256,512]{0,1:T(8,128)(2,1)S(1)} %get-tuple-element.287), channel_id=1, source_target_pairs={{0,1},{1,2},{2,3},{3,4},{4,5},{5,6},{6,7},{7,8},{8,9},{9,10},{10,1... | collective-permute-start | bytes 786440 | tf_op jit(solution)/shard_map/ppermute | solution.py:41
  65.1 21.1 %collective-permute-done.2 = bf16[256,512]{0,1:T(8,128)(2,1)} collective-permute-done((bf16[256,512]{0,1:T(8,128)(2,1)}, bf16[256,512]{0,1:T(8,128)(2,1)}, u32[]{:S(2)}, u32[]{:S(2)}) %collective-permute-start.2) | collective-permute-done | bytes 262176 | tf_op jit(solution)/shard_map/ppermute | solution.py:41
  86.1 2.8 %collective-permute-done.3 = bf16[256,512]{0,1:T(8,128)(2,1)} collective-permute-done((bf16[256,512]{0,1:T(8,128)(2,1)S(1)}, bf16[256,512]{0,1:T(8,128)(2,1)}, u32[]{:S(2)}, u32[]{:S(2)}) %collective-permute-start.3) | collective-permute-done | bytes 262176 | tf_op jit(solution)/shard_map/ppermute | solution.py:41
  88.9 1.3 fusion.32
  90.3 3.5 %fusion.26 = bf16[256,4096]{1,0:T(8,128)(2,1)S(1)} fusion(bf16[256,4096]{1,0:T(8,128)(2,1)} %collective-permute-done.4, s32[]{:T(128)S(6)} %select_n.93, bf16[512,4096]{1,0:T(8,128)(2,1)} %param.7, pred[256]{0:T(512)(128)(4,1)S(1)} %iota_compare_fusion.1), kind=kLoop, calls=%fused_computation.35 | loop fusion | flops 1048576 | bytes 8388868 | tf_op jit(solution)/shard_map/jit(_where)/select_n | solution.py:110
  94.3 2.3 %fusion.18 = (f32[4,8,256]{2,1,0:T(8,128)S(1)}, f32[4,256,256,8]{2,1,3,0:T(8,128)S(1)}) fusion(pred[256,256]{0,1:T(8,128)(4,1)S(1)} %compare_and_fusion.1, bf16[256,4,128,1]{0,2,3,1:T(8,128)(2,1)S(1)} %bitcast.115, bf16[256,4,8,128]{3,2,1,0:T(8,128)(2,1)S(1)} %bitcast.112), kind=kOutput, calls=%fused_computation.25 | convolution fusion | flops 543154176 | bytes 10846208 | tf_op jit(solution)/shard_map/qhgd,khd->hgqk/dot_general | solution.py:55
  96.6 1.8 fusion.17
  98.4 4.3 %bitcast_add_fusion.1 = f32[256,4,8,128]{0,3,2,1:T(8,128)} fusion(f32[256,4,8]{0,2,1:T(8,128)S(1)} %get-tuple-element.283, bf16[256,4,128,1]{0,2,3,1:T(8,128)(2,1)S(1)} %bitcast.114, f32[4,256,256,8]{2,1,3,0:T(8,128)S(1)} %get-tuple-element.290, f32[4,8,256]{2,1,0:T(8,128)S(1)} %broadcast_maximum_fusion, pred[256,256]{0,1:T(8,128)(4,1)S(1)} %compare_and_fusion.1), kind=kOutput, calls=%fused_computation.30 | convolution fusion | flops 546308096 | bytes 12976128 | tf_op jit(solution)/shard_map/hgqk,khd->qhgd/dot_general | solution.py:66
  102.7 76.1 %while.23 = (s32[]{:T(128)}, bf16[256,512]{0,1:T(8,128)(2,1)S(1)}, bf16[256,512]{0,1:T(8,128)(2,1)S(1)}, f32[4,8,256]{2,1,0:T(8,128)S(1)}, f32[4,8,256]{2,1,0:T(...) while((s32[]{:T(128)}, bf16[256,512]{0,1:T(8,128)(2,1)S(1)}, ...), condition=%wide.region_6.7_spmd, body=%wide.region_3.6_spmd.sunk | while | flops 1099129344 | bytes 94642712 | solution.py:130
  102.7 1.9 %collective-permute-start = (bf16[256,512]{0,1:T(8,128)(2,1)S(1)}, bf16[256,512]{0,1:T(8,128)(2,1)S(1)}, u32[]{:S(2)}, u32[]{:S(2)}) collective-permute-start(bf16[256,512]{0,1:T(8,128)(2,1)S(1)} %get-tuple-element.388), channel_id=1, source_target_pairs={{0,1},{1,2},{2,3},{3,4},{4,5},{5,6},{6,7},{7,8},{8,9},{9,10},{10,1... | collective-permute-start | bytes 786440 | tf_op jit(solution)/shard_map/while/body/eval_jaxpr/ppermute | solution.py:41
  104.6 2.0 %collective-permute-start.1 = (bf16[256,512]{0,1:T(8,128)(2,1)S(1)}, bf16[256,512]{0,1:T(8,128)(2,1)S(1)}, u32[]{:S(2)}, u32[]{:S(2)}) collective-permute-start(bf16[256,512]{0,1:T(8,128)(2,1)S(1)} %get-tuple-element.389), channel_id=1, source_target_pairs={{0,1},{1,2},{2,3},{3,4},{4,5},{5,6},{6,7},{7,8},{8,9},{9,10},{10,1... | collective-permute-start | bytes 786440 | tf_op jit(solution)/shard_map/while/body/eval_jaxpr/ppermute | solution.py:41
  106.6 2.1 %copy.55 = bf16[32,8,32,128]{3,2,1,0:T(8,128)(2,1)S(1)} copy(bf16[32,8,32,128]{3,1,2,0:T(8,128)(2,1)} %bitcast.108) | data formatting | bytes 4194304 | tf_op jit(solution)/shard_map/while
  109.6 2.9 %collective-permute-done = bf16[256,512]{0,1:T(8,128)(2,1)S(1)} collective-permute-done((bf16[256,512]{0,1:T(8,128)(2,1)S(1)}, bf16[256,512]{0,1:T(8,128)(2,1)S(1)}, u32[]{:S(2)}, u32[]{:S(2)}) %collective-permute-start) | collective-permute-done | bytes 262176 | tf_op jit(solution)/shard_map/while/body/eval_jaxpr/ppermute | solution.py:41
  112.5 2.3 %fusion.51 = (f32[4,8,256]{2,1,0:T(8,128)S(1)}, f32[4,256,256,8]{2,1,3,0:T(8,128)S(1)}) fusion(pred[256,256]{0,1:T(8,128)(4,1)S(1)} %compare_and_fusion.3, bf16[256,4,128,1]{0,2,3,1:T(8,128)(2,1)S(1)} %bitcast.110, bf16[256,4,8,128]{3,2,1,0:T(8,128)(2,1)S(1)} %bitcast.103), kind=kOutput, calls=%fused_computation.4.clone.1 | convolution fusion | flops 543154176 | bytes 10846208 | tf_op jit(solution)/shard_map/while/body/eval_jaxpr/qhgd,khd->hgqk/dot_general | solution.py:55
  114.8 1.8 fusion.53
  117.0 2.7 %bitcast_add_fusion.3 = f32[256,4,8,128]{0,3,2,1:T(8,128)S(1)} fusion(f32[256,4,8,128]{0,3,2,1:T(8,128)S(1)} %bitcast.105, f32[256,4,8]{0,2,1:T(8,128)S(1)} %get-tuple-element.369, bf16[256,4,128,1]{0,2,3,1:T(8,128)(2,1)S(1)} %bitcast.109, f32[4,256,256,8]{2,1,3,0:T(8,128)S(1)} %get-tuple-element.368, f32[4,8,256]{2,1,0:T(8,128)S(1)} %get-tuple-element.407, ...), kind=kOutput, calls=%fused_computation.6.clone.1 | convolution fusion | flops 547356672 | bytes 17170432 | tf_op jit(solution)/shard_map/while/body/eval_jaxpr/hgqk,khd->qhgd/dot_general | solution.py:66
  119.8 1.9 copy-done.1
  121.7 1.9 %collective-permute-start = (bf16[256,512]{0,1:T(8,128)(2,1)S(1)}, bf16[256,512]{0,1:T(8,128)(2,1)S(1)}, u32[]{:S(2)}, u32[]{:S(2)}) collective-permute-start(bf16[256,512]{0,1:T(8,128)(2,1)S(1)} %get-tuple-element.388), channel_id=1, source_target_pairs={{0,1},{1,2},{2,3},{3,4},{4,5},{5,6},{6,7},{7,8},{8,9},{9,10},{10,1... | collective-permute-start | bytes 786440 | tf_op jit(solution)/shard_map/while/body/eval_jaxpr/ppermute | solution.py:41
  123.6 2.0 %collective-permute-start.1 = (bf16[256,512]{0,1:T(8,128)(2,1)S(1)}, bf16[256,512]{0,1:T(8,128)(2,1)S(1)}, u32[]{:S(2)}, u32[]{:S(2)}) collective-permute-start(bf16[256,512]{0,1:T(8,128)(2,1)S(1)} %get-tuple-element.389), channel_id=1, source_target_pairs={{0,1},{1,2},{2,3},{3,4},{4,5},{5,6},{6,7},{7,8},{8,9},{9,10},{10,1... | collective-permute-start | bytes 786440 | tf_op jit(solution)/shard_map/while/body/eval_jaxpr/ppermute | solution.py:41
  125.6 2.1 %copy.55 = bf16[32,8,32,128]{3,2,1,0:T(8,128)(2,1)S(1)} copy(bf16[32,8,32,128]{3,1,2,0:T(8,128)(2,1)} %bitcast.108) | data formatting | bytes 4194304 | tf_op jit(solution)/shard_map/while
  128.6 2.9 %collective-permute-done = bf16[256,512]{0,1:T(8,128)(2,1)S(1)} collective-permute-done((bf16[256,512]{0,1:T(8,128)(2,1)S(1)}, bf16[256,512]{0,1:T(8,128)(2,1)S(1)}, u32[]{:S(2)}, u32[]{:S(2)}) %collective-permute-start) | collective-permute-done | bytes 262176 | tf_op jit(solution)/shard_map/while/body/eval_jaxpr/ppermute | solution.py:41
  131.5 2.3 %fusion.51 = (f32[4,8,256]{2,1,0:T(8,128)S(1)}, f32[4,256,256,8]{2,1,3,0:T(8,128)S(1)}) fusion(pred[256,256]{0,1:T(8,128)(4,1)S(1)} %compare_and_fusion.3, bf16[256,4,128,1]{0,2,3,1:T(8,128)(2,1)S(1)} %bitcast.110, bf16[256,4,8,128]{3,2,1,0:T(8,128)(2,1)S(1)} %bitcast.103), kind=kOutput, calls=%fused_computation.4.clone.1 | convolution fusion | flops 543154176 | bytes 10846208 | tf_op jit(solution)/shard_map/while/body/eval_jaxpr/qhgd,khd->hgqk/dot_general | solution.py:55
  133.9 1.8 fusion.53
  136.0 2.7 %bitcast_add_fusion.3 = f32[256,4,8,128]{0,3,2,1:T(8,128)S(1)} fusion(f32[256,4,8,128]{0,3,2,1:T(8,128)S(1)} %bitcast.105, f32[256,4,8]{0,2,1:T(8,128)S(1)} %get-tuple-element.369, bf16[256,4,128,1]{0,2,3,1:T(8,128)(2,1)S(1)} %bitcast.109, f32[4,256,256,8]{2,1,3,0:T(8,128)S(1)} %get-tuple-element.368, f32[4,8,256]{2,1,0:T(8,128)S(1)} %get-tuple-element.407, ...), kind=kOutput, calls=%fused_computation.6.clone.1 | convolution fusion | flops 547356672 | bytes 17170432 | tf_op jit(solution)/shard_map/while/body/eval_jaxpr/hgqk,khd->qhgd/dot_general | solution.py:66
  138.8 1.9 copy-done.1
  140.7 1.9 %collective-permute-start = (bf16[256,512]{0,1:T(8,128)(2,1)S(1)}, bf16[256,512]{0,1:T(8,128)(2,1)S(1)}, u32[]{:S(2)}, u32[]{:S(2)}) collective-permute-start(bf16[256,512]{0,1:T(8,128)(2,1)S(1)} %get-tuple-element.388), channel_id=1, source_target_pairs={{0,1},{1,2},{2,3},{3,4},{4,5},{5,6},{6,7},{7,8},{8,9},{9,10},{10,1... | collective-permute-start | bytes 786440 | tf_op jit(solution)/shard_map/while/body/eval_jaxpr/ppermute | solution.py:41
  142.7 2.0 %collective-permute-start.1 = (bf16[256,512]{0,1:T(8,128)(2,1)S(1)}, bf16[256,512]{0,1:T(8,128)(2,1)S(1)}, u32[]{:S(2)}, u32[]{:S(2)}) collective-permute-start(bf16[256,512]{0,1:T(8,128)(2,1)S(1)} %get-tuple-element.389), channel_id=1, source_target_pairs={{0,1},{1,2},{2,3},{3,4},{4,5},{5,6},{6,7},{7,8},{8,9},{9,10},{10,1... | collective-permute-start | bytes 786440 | tf_op jit(solution)/shard_map/while/body/eval_jaxpr/ppermute | solution.py:41
  144.7 2.1 %copy.55 = bf16[32,8,32,128]{3,2,1,0:T(8,128)(2,1)S(1)} copy(bf16[32,8,32,128]{3,1,2,0:T(8,128)(2,1)} %bitcast.108) | data formatting | bytes 4194304 | tf_op jit(solution)/shard_map/while
  147.7 2.9 %collective-permute-done = bf16[256,512]{0,1:T(8,128)(2,1)S(1)} collective-permute-done((bf16[256,512]{0,1:T(8,128)(2,1)S(1)}, bf16[256,512]{0,1:T(8,128)(2,1)S(1)}, u32[]{:S(2)}, u32[]{:S(2)}) %collective-permute-start) | collective-permute-done | bytes 262176 | tf_op jit(solution)/shard_map/while/body/eval_jaxpr/ppermute | solution.py:41
  150.5 2.3 %fusion.51 = (f32[4,8,256]{2,1,0:T(8,128)S(1)}, f32[4,256,256,8]{2,1,3,0:T(8,128)S(1)}) fusion(pred[256,256]{0,1:T(8,128)(4,1)S(1)} %compare_and_fusion.3, bf16[256,4,128,1]{0,2,3,1:T(8,128)(2,1)S(1)} %bitcast.110, bf16[256,4,8,128]{3,2,1,0:T(8,128)(2,1)S(1)} %bitcast.103), kind=kOutput, calls=%fused_computation.4.clone.1 | convolution fusion | flops 543154176 | bytes 10846208 | tf_op jit(solution)/shard_map/while/body/eval_jaxpr/qhgd,khd->hgqk/dot_general | solution.py:55
  152.9 1.8 fusion.53
  155.1 2.7 %bitcast_add_fusion.3 = f32[256,4,8,128]{0,3,2,1:T(8,128)S(1)} fusion(f32[256,4,8,128]{0,3,2,1:T(8,128)S(1)} %bitcast.105, f32[256,4,8]{0,2,1:T(8,128)S(1)} %get-tuple-element.369, bf16[256,4,128,1]{0,2,3,1:T(8,128)(2,1)S(1)} %bitcast.109, f32[4,256,256,8]{2,1,3,0:T(8,128)S(1)} %get-tuple-element.368, f32[4,8,256]{2,1,0:T(8,128)S(1)} %get-tuple-element.407, ...), kind=kOutput, calls=%fused_computation.6.clone.1 | convolution fusion | flops 547356672 | bytes 17170432 | tf_op jit(solution)/shard_map/while/body/eval_jaxpr/hgqk,khd->qhgd/dot_general | solution.py:66
  157.8 1.9 copy-done.1
  159.7 1.9 %collective-permute-start = (bf16[256,512]{0,1:T(8,128)(2,1)S(1)}, bf16[256,512]{0,1:T(8,128)(2,1)S(1)}, u32[]{:S(2)}, u32[]{:S(2)}) collective-permute-start(bf16[256,512]{0,1:T(8,128)(2,1)S(1)} %get-tuple-element.388), channel_id=1, source_target_pairs={{0,1},{1,2},{2,3},{3,4},{4,5},{5,6},{6,7},{7,8},{8,9},{9,10},{10,1... | collective-permute-start | bytes 786440 | tf_op jit(solution)/shard_map/while/body/eval_jaxpr/ppermute | solution.py:41
  161.7 2.0 %collective-permute-start.1 = (bf16[256,512]{0,1:T(8,128)(2,1)S(1)}, bf16[256,512]{0,1:T(8,128)(2,1)S(1)}, u32[]{:S(2)}, u32[]{:S(2)}) collective-permute-start(bf16[256,512]{0,1:T(8,128)(2,1)S(1)} %get-tuple-element.389), channel_id=1, source_target_pairs={{0,1},{1,2},{2,3},{3,4},{4,5},{5,6},{6,7},{7,8},{8,9},{9,10},{10,1... | collective-permute-start | bytes 786440 | tf_op jit(solution)/shard_map/while/body/eval_jaxpr/ppermute | solution.py:41
  163.7 2.1 %copy.55 = bf16[32,8,32,128]{3,2,1,0:T(8,128)(2,1)S(1)} copy(bf16[32,8,32,128]{3,1,2,0:T(8,128)(2,1)} %bitcast.108) | data formatting | bytes 4194304 | tf_op jit(solution)/shard_map/while
  166.7 2.9 %collective-permute-done = bf16[256,512]{0,1:T(8,128)(2,1)S(1)} collective-permute-done((bf16[256,512]{0,1:T(8,128)(2,1)S(1)}, bf16[256,512]{0,1:T(8,128)(2,1)S(1)}, u32[]{:S(2)}, u32[]{:S(2)}) %collective-permute-start) | collective-permute-done | bytes 262176 | tf_op jit(solution)/shard_map/while/body/eval_jaxpr/ppermute | solution.py:41
  169.5 2.3 %fusion.51 = (f32[4,8,256]{2,1,0:T(8,128)S(1)}, f32[4,256,256,8]{2,1,3,0:T(8,128)S(1)}) fusion(pred[256,256]{0,1:T(8,128)(4,1)S(1)} %compare_and_fusion.3, bf16[256,4,128,1]{0,2,3,1:T(8,128)(2,1)S(1)} %bitcast.110, bf16[256,4,8,128]{3,2,1,0:T(8,128)(2,1)S(1)} %bitcast.103), kind=kOutput, calls=%fused_computation.4.clone.1 | convolution fusion | flops 543154176 | bytes 10846208 | tf_op jit(solution)/shard_map/while/body/eval_jaxpr/qhgd,khd->hgqk/dot_general | solution.py:55
  171.9 1.8 fusion.53
  174.1 2.7 %bitcast_add_fusion.3 = f32[256,4,8,128]{0,3,2,1:T(8,128)S(1)} fusion(f32[256,4,8,128]{0,3,2,1:T(8,128)S(1)} %bitcast.105, f32[256,4,8]{0,2,1:T(8,128)S(1)} %get-tuple-element.369, bf16[256,4,128,1]{0,2,3,1:T(8,128)(2,1)S(1)} %bitcast.109, f32[4,256,256,8]{2,1,3,0:T(8,128)S(1)} %get-tuple-element.368, f32[4,8,256]{2,1,0:T(8,128)S(1)} %get-tuple-element.407, ...), kind=kOutput, calls=%fused_computation.6.clone.1 | convolution fusion | flops 547356672 | bytes 17170432 | tf_op jit(solution)/shard_map/while/body/eval_jaxpr/hgqk,khd->qhgd/dot_general | solution.py:66
  176.9 1.9 copy-done.1
  178.8 5.7 %copy.29 = f32[256,4096]{1,0:T(8,128)} copy(f32[256,4096]{0,1:T(8,128)} %get-tuple-element.242) | data formatting | bytes 8388608 | tf_op jit(solution)/shard_map/while | solution.py:130
  186.7 4.0 %fusion.21 = bf16[256,4096]{1,0:T(8,128)(2,1)} fusion(f32[256,4096]{1,0:T(8,128)S(1)} %copy-done.4, f32[32,8,32,128]{3,2,1,0:T(8,128)S(1)} %bitcast.111), kind=kLoop, calls=%fused_computation.29 | loop fusion | flops 2097152 | bytes 10485760 | tf_op jit(solution)/shard_map/convert_element_type | solution.py:85
  (94 shorter events, 15.6 us)
Async XLA Ops:
  0.0 55.8 %copy-start.7 = (bf16[512,512]{1,0:T(8,128)(2,1)S(1)}, bf16[512,512]{1,0:T(8,128)(2,1)}, u32[]{:S(2)}) copy-start(bf16[512,512]{1,0:T(8,128)(2,1)} %param.8) | copy-start | bytes 1572868
  53.7 36.6 %collective-permute-start.4 = (bf16[256,4096]{1,0:T(8,128)(2,1)S(1)}, bf16[256,4096]{1,0:T(8,128)(2,1)}, u32[]{:S(2)}, u32[]{:S(2)}) collective-permute-start(bf16[256,4096]{1,0:T(8,128)(2,1)S(1)} %dynamic-slice_select_fusion), channel_id=1, source_target_pairs={{0,1},{1,2},{2,3},{3,4},{4,5},{5,6},{6,7},{7,8},{8,9},{9,10},{10,1... | collective-permute-start | bytes 6291464 | tf_op jit(solution)/shard_map/ppermute | solution.py:41
  58.3 27.9 %collective-permute-start.2 = (bf16[256,512]{0,1:T(8,128)(2,1)}, bf16[256,512]{0,1:T(8,128)(2,1)}, u32[]{:S(2)}, u32[]{:S(2)}) collective-permute-start(bf16[256,512]{0,1:T(8,128)(2,1)} %get-tuple-element.288), channel_id=1, source_target_pairs={{0,1},{1,2},{2,3},{3,4},{4,5},{5,6},{6,7},{7,8},{8,9},{9,10},{10,1... | collective-permute-start | bytes 786440 | tf_op jit(solution)/shard_map/ppermute | solution.py:41
  62.0 26.9 %collective-permute-start.3 = (bf16[256,512]{0,1:T(8,128)(2,1)S(1)}, bf16[256,512]{0,1:T(8,128)(2,1)}, u32[]{:S(2)}, u32[]{:S(2)}) collective-permute-start(bf16[256,512]{0,1:T(8,128)(2,1)S(1)} %get-tuple-element.287), channel_id=1, source_target_pairs={{0,1},{1,2},{2,3},{3,4},{4,5},{5,6},{6,7},{7,8},{8,9},{9,10},{10,1... | collective-permute-start | bytes 786440 | tf_op jit(solution)/shard_map/ppermute | solution.py:41
  90.3 4.0 %copy-start.5 = (bf16[256,512]{0,1:T(8,128)(2,1)}, bf16[256,512]{0,1:T(8,128)(2,1)S(1)}, u32[]{:S(2)}) copy-start(bf16[256,512]{0,1:T(8,128)(2,1)S(1)} %get-tuple-element.371) | copy-start | bytes 786436
  98.4 4.3 %copy-start.6 = (bf16[256,512]{0,1:T(8,128)(2,1)S(1)}, bf16[256,512]{0,1:T(8,128)(2,1)}, u32[]{:S(2)}) copy-start(bf16[256,512]{0,1:T(8,128)(2,1)} %copy-done.5) | copy-start | bytes 786436
  102.7 3.9 %copy-start.2 = (bf16[256,4096]{1,0:T(8,128)(2,1)}, bf16[256,4096]{1,0:T(8,128)(2,1)S(1)}, u32[]{:S(2)}) copy-start(bf16[256,4096]{1,0:T(8,128)(2,1)S(1)} %get-tuple-element.414) | copy-start | bytes 6291460 | tf_op jit(solution)/shard_map/while
  102.7 9.8 %collective-permute-start = (bf16[256,512]{0,1:T(8,128)(2,1)S(1)}, bf16[256,512]{0,1:T(8,128)(2,1)S(1)}, u32[]{:S(2)}, u32[]{:S(2)}) collective-permute-start(bf16[256,512]{0,1:T(8,128)(2,1)S(1)} %get-tuple-element.388), channel_id=1, source_target_pairs={{0,1},{1,2},{2,3},{3,4},{4,5},{5,6},{6,7},{7,8},{8,9},{9,10},{10,1... | collective-permute-start | bytes 786440 | tf_op jit(solution)/shard_map/while/body/eval_jaxpr/ppermute | solution.py:41
  104.6 12.1 %collective-permute-start.1 = (bf16[256,512]{0,1:T(8,128)(2,1)S(1)}, bf16[256,512]{0,1:T(8,128)(2,1)S(1)}, u32[]{:S(2)}, u32[]{:S(2)}) collective-permute-start(bf16[256,512]{0,1:T(8,128)(2,1)S(1)} %get-tuple-element.389), channel_id=1, source_target_pairs={{0,1},{1,2},{2,3},{3,4},{4,5},{5,6},{6,7},{7,8},{8,9},{9,10},{10,1... | collective-permute-start | bytes 786440 | tf_op jit(solution)/shard_map/while/body/eval_jaxpr/ppermute | solution.py:41
  114.8 2.2 %copy-start = (f32[256,4096]{0,1:T(8,128)S(1)}, f32[256,4096]{0,1:T(8,128)}, u32[]{:S(2)}) copy-start(f32[256,4096]{0,1:T(8,128)} %get-tuple-element.392) | copy-start | bytes 12582916 | tf_op jit(solution)/shard_map/while
  117.0 4.7 %copy-start.3 = (bf16[256,4096]{1,0:T(8,128)(2,1)S(1)}, bf16[256,4096]{1,0:T(8,128)(2,1)}, u32[]{:S(2)}) copy-start(bf16[256,4096]{1,0:T(8,128)(2,1)} %copy-done.2) | copy-start | bytes 6291460 | tf_op jit(solution)/shard_map/while
  119.8 1.9 %copy-start.1 = (f32[256,4,8,128]{0,3,2,1:T(8,128)}, f32[256,4,8,128]{0,3,2,1:T(8,128)S(1)}, u32[]{:S(2)}) copy-start(f32[256,4,8,128]{0,3,2,1:T(8,128)S(1)} %bitcast_add_fusion.3) | copy-start | bytes 12582916 | tf_op jit(solution)/shard_map/while
  121.7 3.9 %copy-start.2 = (bf16[256,4096]{1,0:T(8,128)(2,1)}, bf16[256,4096]{1,0:T(8,128)(2,1)S(1)}, u32[]{:S(2)}) copy-start(bf16[256,4096]{1,0:T(8,128)(2,1)S(1)} %get-tuple-element.414) | copy-start | bytes 6291460 | tf_op jit(solution)/shard_map/while
  121.7 9.8 %collective-permute-start = (bf16[256,512]{0,1:T(8,128)(2,1)S(1)}, bf16[256,512]{0,1:T(8,128)(2,1)S(1)}, u32[]{:S(2)}, u32[]{:S(2)}) collective-permute-start(bf16[256,512]{0,1:T(8,128)(2,1)S(1)} %get-tuple-element.388), channel_id=1, source_target_pairs={{0,1},{1,2},{2,3},{3,4},{4,5},{5,6},{6,7},{7,8},{8,9},{9,10},{10,1... | collective-permute-start | bytes 786440 | tf_op jit(solution)/shard_map/while/body/eval_jaxpr/ppermute | solution.py:41
  123.6 12.1 %collective-permute-start.1 = (bf16[256,512]{0,1:T(8,128)(2,1)S(1)}, bf16[256,512]{0,1:T(8,128)(2,1)S(1)}, u32[]{:S(2)}, u32[]{:S(2)}) collective-permute-start(bf16[256,512]{0,1:T(8,128)(2,1)S(1)} %get-tuple-element.389), channel_id=1, source_target_pairs={{0,1},{1,2},{2,3},{3,4},{4,5},{5,6},{6,7},{7,8},{8,9},{9,10},{10,1... | collective-permute-start | bytes 786440 | tf_op jit(solution)/shard_map/while/body/eval_jaxpr/ppermute | solution.py:41
  133.8 2.2 %copy-start = (f32[256,4096]{0,1:T(8,128)S(1)}, f32[256,4096]{0,1:T(8,128)}, u32[]{:S(2)}) copy-start(f32[256,4096]{0,1:T(8,128)} %get-tuple-element.392) | copy-start | bytes 12582916 | tf_op jit(solution)/shard_map/while
  136.0 4.7 %copy-start.3 = (bf16[256,4096]{1,0:T(8,128)(2,1)S(1)}, bf16[256,4096]{1,0:T(8,128)(2,1)}, u32[]{:S(2)}) copy-start(bf16[256,4096]{1,0:T(8,128)(2,1)} %copy-done.2) | copy-start | bytes 6291460 | tf_op jit(solution)/shard_map/while
  138.8 1.9 %copy-start.1 = (f32[256,4,8,128]{0,3,2,1:T(8,128)}, f32[256,4,8,128]{0,3,2,1:T(8,128)S(1)}, u32[]{:S(2)}) copy-start(f32[256,4,8,128]{0,3,2,1:T(8,128)S(1)} %bitcast_add_fusion.3) | copy-start | bytes 12582916 | tf_op jit(solution)/shard_map/while
  140.7 3.9 %copy-start.2 = (bf16[256,4096]{1,0:T(8,128)(2,1)}, bf16[256,4096]{1,0:T(8,128)(2,1)S(1)}, u32[]{:S(2)}) copy-start(bf16[256,4096]{1,0:T(8,128)(2,1)S(1)} %get-tuple-element.414) | copy-start | bytes 6291460 | tf_op jit(solution)/shard_map/while
  140.7 9.8 %collective-permute-start = (bf16[256,512]{0,1:T(8,128)(2,1)S(1)}, bf16[256,512]{0,1:T(8,128)(2,1)S(1)}, u32[]{:S(2)}, u32[]{:S(2)}) collective-permute-start(bf16[256,512]{0,1:T(8,128)(2,1)S(1)} %get-tuple-element.388), channel_id=1, source_target_pairs={{0,1},{1,2},{2,3},{3,4},{4,5},{5,6},{6,7},{7,8},{8,9},{9,10},{10,1... | collective-permute-start | bytes 786440 | tf_op jit(solution)/shard_map/while/body/eval_jaxpr/ppermute | solution.py:41
  142.7 12.1 %collective-permute-start.1 = (bf16[256,512]{0,1:T(8,128)(2,1)S(1)}, bf16[256,512]{0,1:T(8,128)(2,1)S(1)}, u32[]{:S(2)}, u32[]{:S(2)}) collective-permute-start(bf16[256,512]{0,1:T(8,128)(2,1)S(1)} %get-tuple-element.389), channel_id=1, source_target_pairs={{0,1},{1,2},{2,3},{3,4},{4,5},{5,6},{6,7},{7,8},{8,9},{9,10},{10,1... | collective-permute-start | bytes 786440 | tf_op jit(solution)/shard_map/while/body/eval_jaxpr/ppermute | solution.py:41
  152.9 2.2 %copy-start = (f32[256,4096]{0,1:T(8,128)S(1)}, f32[256,4096]{0,1:T(8,128)}, u32[]{:S(2)}) copy-start(f32[256,4096]{0,1:T(8,128)} %get-tuple-element.392) | copy-start | bytes 12582916 | tf_op jit(solution)/shard_map/while
  155.1 4.7 %copy-start.3 = (bf16[256,4096]{1,0:T(8,128)(2,1)S(1)}, bf16[256,4096]{1,0:T(8,128)(2,1)}, u32[]{:S(2)}) copy-start(bf16[256,4096]{1,0:T(8,128)(2,1)} %copy-done.2) | copy-start | bytes 6291460 | tf_op jit(solution)/shard_map/while
  157.8 1.9 %copy-start.1 = (f32[256,4,8,128]{0,3,2,1:T(8,128)}, f32[256,4,8,128]{0,3,2,1:T(8,128)S(1)}, u32[]{:S(2)}) copy-start(f32[256,4,8,128]{0,3,2,1:T(8,128)S(1)} %bitcast_add_fusion.3) | copy-start | bytes 12582916 | tf_op jit(solution)/shard_map/while
  159.7 3.9 %copy-start.2 = (bf16[256,4096]{1,0:T(8,128)(2,1)}, bf16[256,4096]{1,0:T(8,128)(2,1)S(1)}, u32[]{:S(2)}) copy-start(bf16[256,4096]{1,0:T(8,128)(2,1)S(1)} %get-tuple-element.414) | copy-start | bytes 6291460 | tf_op jit(solution)/shard_map/while
  159.7 9.8 %collective-permute-start = (bf16[256,512]{0,1:T(8,128)(2,1)S(1)}, bf16[256,512]{0,1:T(8,128)(2,1)S(1)}, u32[]{:S(2)}, u32[]{:S(2)}) collective-permute-start(bf16[256,512]{0,1:T(8,128)(2,1)S(1)} %get-tuple-element.388), channel_id=1, source_target_pairs={{0,1},{1,2},{2,3},{3,4},{4,5},{5,6},{6,7},{7,8},{8,9},{9,10},{10,1... | collective-permute-start | bytes 786440 | tf_op jit(solution)/shard_map/while/body/eval_jaxpr/ppermute | solution.py:41
  161.7 12.1 %collective-permute-start.1 = (bf16[256,512]{0,1:T(8,128)(2,1)S(1)}, bf16[256,512]{0,1:T(8,128)(2,1)S(1)}, u32[]{:S(2)}, u32[]{:S(2)}) collective-permute-start(bf16[256,512]{0,1:T(8,128)(2,1)S(1)} %get-tuple-element.389), channel_id=1, source_target_pairs={{0,1},{1,2},{2,3},{3,4},{4,5},{5,6},{6,7},{7,8},{8,9},{9,10},{10,1... | collective-permute-start | bytes 786440 | tf_op jit(solution)/shard_map/while/body/eval_jaxpr/ppermute | solution.py:41
  171.9 2.2 %copy-start = (f32[256,4096]{0,1:T(8,128)S(1)}, f32[256,4096]{0,1:T(8,128)}, u32[]{:S(2)}) copy-start(f32[256,4096]{0,1:T(8,128)} %get-tuple-element.392) | copy-start | bytes 12582916 | tf_op jit(solution)/shard_map/while
  174.1 4.7 %copy-start.3 = (bf16[256,4096]{1,0:T(8,128)(2,1)S(1)}, bf16[256,4096]{1,0:T(8,128)(2,1)}, u32[]{:S(2)}) copy-start(bf16[256,4096]{1,0:T(8,128)(2,1)} %copy-done.2) | copy-start | bytes 6291460 | tf_op jit(solution)/shard_map/while
  176.8 1.9 %copy-start.1 = (f32[256,4,8,128]{0,3,2,1:T(8,128)}, f32[256,4,8,128]{0,3,2,1:T(8,128)S(1)}, u32[]{:S(2)}) copy-start(f32[256,4,8,128]{0,3,2,1:T(8,128)S(1)} %bitcast_add_fusion.3) | copy-start | bytes 12582916 | tf_op jit(solution)/shard_map/while
  184.5 2.2 %copy-start.4 = (f32[256,4096]{1,0:T(8,128)S(1)}, f32[256,4096]{1,0:T(8,128)}, u32[]{:S(2)}) copy-start(f32[256,4096]{1,0:T(8,128)} %copy.29) | copy-start | bytes 12582916
where the time goes:
time: 193 us; the launch traced here: 191 us
  blocking collectives  45.3 us (23%)
  waiting for transfers between devices  35.4 us (18%)
  local copies, waits for them, and re-layouts  34.6 us (18%)
  matrix products  26.6 us (14%)
  starting transfers between devices  23.5 us (12%)
  other arithmetic  22.6 us (12%)
  between operations  2.04 us (1%)
    unnamed x2, blocking collectives  45.3 us
    ppermute x11, waiting for transfers between devices, passed_along(): return lax.ppermute(block, axis, route)  35.4 us
    ppermute x11, starting transfers between devices, passed_along(): return lax.ppermute(block, axis, route)  23.5 us
    while x48, local copies, waits for them, and re-layouts  17.3 us
    dot_general x5, matrix products, attend_block(): jnp.einsum('hgqk,khd->qhgd', weights.astype(jnp.bfloat16), value_rows.res...  15.1 us
    dot_general x5, matrix products, attend_block(): jnp.einsum('qhgd,khd->hgqk', query_rows.reshape(SPAN, KV_HEADS, groups, H...  11.5 us
    reduce_sum x5, other arithmetic, attend_block(): totals = totals * factor + jnp.sum(weights, axis=-1)  8.95 us
    unnamed x17, local copies, waits for them, and re-layouts  6.44 us
  transfers between devices with their start and end apart: 11, of which 6 were waited for; matrix products, arithmetic and copies ran while one was open for 17% of the time, Pallas kernels for 0%

commit v1 on v0

v1 whole, which is shorter than its diff:
```python
import functools
import math

import jax
import jax.numpy as jnp
from jax import lax
from jax.experimental import pallas as pl
from jax.experimental.pallas import tpu as pltpu
from jax.sharding import PartitionSpec as P

KV_HEADS = 4
HEAD_DIM = 128
SPAN = 256
WINDOW = 5
X, Z = 4, 16
MESH = pl.DeviceIdType.MESH
SCALE = math.log2(math.e) / math.sqrt(HEAD_DIM)
MASKED = -1e30
BF16, F32, I32 = jnp.bfloat16, jnp.float32, jnp.int32


def kernel(
    q_hbm,
    k_hbm,
    v_hbm,
    count_ref,
    seg_hbm,
    out_hbm,
    qf,
    kvf,
    seg,
    count,
    count_prev,
    count_pair,
    pair_sum,
    column,
    column_sum,
    columns,
    base,
    base_in,
    before,
    before_in,
    lead,
    turn,
    kv_tail,
    kv_tail_in,
    q_tail,
    q_tail_in,
    kv,
    qr,
    bias,
    out,
    acc,
    top,
    total,
    load_sem,
    seg_sem,
    out_sem,
    one_send,
    one_recv,
    z_send,
    z_recv,
    x_send,
    x_recv,
    tail_send,
    tail_recv,
    block_send,
    block_recv,
):
    n = lax.axis_size("seq")
    d = lax.axis_index("seq")
    core = lax.rem(d, 2)
    chip = d // 2
    z = lax.rem(chip, Z)
    x = chip // Z
    heads = qr.shape[0] // KV_HEADS
    wide = heads * HEAD_DIM

    def at(index):
        return {"seq": lax.rem(index + n, n)}

    follower = at(d + 1)
    onward = at(d + 2)
    partner = at(d + 1 - 2 * core)

    def remote(src, dst, send, recv, device):
        return pltpu.make_async_remote_copy(
            src_ref=src,
            dst_ref=dst,
            send_sem=send,
            recv_sem=recv,
            device_id=device,
            device_id_type=MESH,
        )

    def z_peer(k):
        return at(x * (2 * Z) + 2 * lax.rem(z + k, Z) + core)

    def x_peer(k):
        return at(lax.rem(x + k, X) * (2 * Z) + 2 * z + core)

    loads = []
    for g in range(KV_HEADS):
        columns_of = pl.ds(g * HEAD_DIM, HEAD_DIM)
        for part, src in enumerate((k_hbm, v_hbm)):
            loads.append(
                pltpu.make_async_copy(
                    src.at[:, columns_of],
                    kvf.at[g, :, pl.ds(part * HEAD_DIM, HEAD_DIM)],
                    load_sem.at[2 * g + part],
                )
            )
    q_loads = [
        pltpu.make_async_copy(
            q_hbm.at[:, pl.ds(g * wide, wide)],
            qf.at[g],
            load_sem.at[2 * KV_HEADS + g],
        )
        for g in range(KV_HEADS)
    ]
    seg_load = pltpu.make_async_copy(seg_hbm, seg, seg_sem)
    for load in loads + q_loads + [seg_load]:
        load.start()

    barrier = pltpu.get_barrier_semaphore()

    def greet(device):
        pl.semaphore_signal(barrier, inc=1, device_id=device, device_id_type=MESH)

    greet(partner)
    greet(at(d + 2))
    greet(at(d - 2))

    @pl.when(core == 1)
    def _():
        greet(at(d + 1))

    @pl.when(core == 0)
    def _():
        greet(at(d - 1))
        lax.fori_loop(1, Z, lambda k, _: greet(z_peer(k)), None)
        lax.fori_loop(1, X, lambda k, _: greet(x_peer(k)), None)

    own_count = count_ref[0]
    count[...] = jnp.full(count.shape, own_count.astype(F32))
    for load in loads:
        load.wait()

    high = own_count - SPAN
    for g in range(KV_HEADS):
        slot = lax.broadcasted_iota(I32, (SPAN, 2 * HEAD_DIM), 0)
        kv_tail[g] = jnp.where(slot < high, kvf[g, SPAN:, :], kvf[g, :SPAN, :])

    def select_q(g):
        q_loads[g].wait()
        slot = lax.broadcasted_iota(I32, (SPAN, wide), 0)
        q_tail[g] = jnp.where(slot < high, qf[g, SPAN:, :], qf[g, :SPAN, :])

    select_q(0)
    pl.semaphore_wait(barrier, jnp.where(core == 0, Z + X + 2, 4))

    count_copy = remote(count, count_prev, one_send.at[0], one_recv.at[0], follower)
    pair_copy = remote(count, count_pair, one_send.at[1], one_recv.at[1], partner)
    before_copy = remote(before, before_in, one_send.at[2], one_recv.at[2], partner)
    has_next, has_prev = d < n - 1, d > 0
    has_onward, has_back = d < n - 2, d > 1

    def start_if(there, copy):
        pl.when(there)(copy.start)

    start_if(has_next, count_copy)
    start_if(core == 1, pair_copy)

    kv_tails = [
        remote(kv_tail.at[g], kv_tail_in.at[g], tail_send.at[g], tail_recv.at[g], follower)
        for g in range(KV_HEADS)
    ]
    q_tails = [
        remote(
            q_tail.at[g],
            q_tail_in.at[g],
            tail_send.at[KV_HEADS + g],
            tail_recv.at[KV_HEADS + g],
            follower,
        )
        for g in range(KV_HEADS)
    ]
    for g in range(KV_HEADS):
        start_if(has_next, kv_tails[g])
    select_q(1)
    start_if(has_next, q_tails[0])
    select_q(2)
    start_if(has_next, q_tails[1])
    select_q(3)
    pl.when(has_prev)(count_copy.wait_recv)

    @pl.when(d == 0)
    def _():
        count_prev[...] = jnp.full(count_prev.shape, float(SPAN), F32)
        kv_tail_in[...] = jnp.zeros(kv_tail_in.shape, BF16)
        q_tail_in[...] = jnp.zeros(q_tail_in.shape, BF16)

    @pl.when(d < 2)
    def _():
        for t in (2, 4):
            kv[:, t] = jnp.zeros((KV_HEADS, *kv.shape[2:]), BF16)

    @pl.when(core == 0)
    def _():
        pair_copy.wait_recv()
        pair_sum[...] = count[...] + count_pair[...]
        column[pl.ds(z, 1)] = pair_sum[...][None]

        def z_copy(k):
            return remote(pair_sum, column.at[z], z_send.at[k], z_recv.at[z], z_peer(k))

        def z_from(k):
            other = lax.rem(z + k, Z)
            return remote(
                pair_sum, column.at[other], z_send.at[k], z_recv.at[other], z_peer(k)
            )

        lax.fori_loop(1, Z, lambda k, _: z_copy(k).start(), None)
        lax.fori_loop(1, Z, lambda k, _: z_from(k).wait_recv(), None)
        z_place = lax.broadcasted_iota(I32, column.shape, 0)
        x_place = lax.broadcasted_iota(I32, columns.shape, 0)
        base_copy = remote(base, base_in, one_send.at[3], one_recv.at[3], z_peer(Z - 1))

        def x_copy(k):
            return remote(column_sum, columns.at[x], x_send.at[k], x_recv.at[x], x_peer(k))

        def x_from(k):
            other = lax.rem(x + k, X)
            return remote(
                column_sum, columns.at[other], x_send.at[k], x_recv.at[other], x_peer(k)
            )

        @pl.when(z > 0)
        def _():
            column_sum[...] = jnp.sum(column[...], axis=0)
            columns[pl.ds(x, 1)] = column_sum[...][None]
            for k in range(1, X):
                x_copy(k).start()
            for k in range(1, X):
                x_from(k).wait_recv()
            base[...] = jnp.sum(jnp.where(x_place < x, columns[...], 0.0), axis=0)
            pl.when(z == 1)(base_copy.start)
            before[...] = base[...] + jnp.sum(jnp.where(z_place < z, column[...], 0.0), axis=0)

        @pl.when(z == 0)
        def _():
            base_copy.wait_recv()
            before[...] = base_in[...]

        before_copy.start()
        lead[...] = before[...] - (d * SPAN).astype(F32)
        lax.fori_loop(1, Z, lambda k, _: z_copy(k).wait_send(), None)

        @pl.when(z > 0)
        def _():
            for k in range(1, X):
                x_copy(k).wait_send()

        pl.when(z == 1)(base_copy.wait_send)
        before_copy.wait_send()

    @pl.when(core == 1)
    def _():
        before_copy.wait_recv()
        lead[...] = before_in[...] + count_prev[...] - (d * SPAN).astype(F32)
        pair_copy.wait_send()

    lead_in = lead[0:1, :].astype(I32)
    lead_before = (lead[0:1, :] - count_prev[0:1, :]).astype(I32)
    place = lax.broadcasted_iota(I32, (SPAN, SPAN), 0)
    slot = lax.broadcasted_iota(I32, (SPAN, SPAN), 1)
    step = place - slot
    arrived = (((step - lead_before) & (SPAN - 1)) == 0) & (place < lead_in)
    turn[:, :SPAN] = jnp.where(arrived, 1.0, 0.0).astype(BF16)
    turn[:, SPAN:] = jnp.where(step == lead_in, 1.0, 0.0).astype(BF16)

    def turned(tail, own):
        rows = jnp.dot(turn[:, :SPAN], tail, preferred_element_type=F32)
        rows += jnp.dot(turn[:, SPAN:], own, preferred_element_type=F32)
        return rows.astype(BF16)

    def hop(g, source, target, device):
        return remote(
            kv.at[g, source],
            kv.at[g, target],
            block_send.at[g, target],
            block_recv.at[g, target],
            device,
        )

    def arrival(g, target):
        hop(g, target, target, partner).wait_recv()

    for g in range(KV_HEADS):
        pl.when(has_prev)(kv_tails[g].wait_recv)
        kv[g, 0] = turned(kv_tail_in[g], kvf[g, :SPAN, :])

    seg_load.wait()
    both = HEAD_DIM

    def clip_row(block):
        row = 2 * jnp.maximum(block, 0)
        return jnp.concatenate([seg[pl.ds(row, 1), :], seg[pl.ds(row + 1, 1), :]], axis=1).astype(F32)

    query_clip = jnp.broadcast_to(clip_row(d), (SPAN, SPAN)).T
    for t in range(WINDOW):
        same = query_clip == clip_row(d - t)
        if t == 0:
            same = same & (slot <= place)
        there = jnp.where(d >= t, 0.0, MASKED)
        bias[:, pl.ds(t * SPAN, SPAN)] = jnp.where(same, 0.0, MASKED) + there

    def send_own(g):
        start_if(has_onward, hop(g, 0, 2, onward))

        @pl.when(core == 0)
        def _():
            hop(g, 0, 1, partner).start()

    def forward(g):
        pl.when(has_back)(lambda: arrival(g, 2))
        start_if(has_onward, hop(g, 2, 4, onward))

        @pl.when(core == 0)
        def _():
            hop(g, 2, 3, partner).start()

        @pl.when(core == 1)
        def _():
            hop(g, 2, 1, partner).start()

    def forward_far(g):
        pl.when(has_back)(lambda: arrival(g, 4))

        @pl.when(core == 1)
        def _():
            hop(g, 4, 3, partner).start()

    send_own(0)
    send_own(1)
    start_if(has_next, q_tails[2])
    send_own(2)
    send_own(3)
    start_if(has_next, q_tails[3])

    def turn_q(g):
        pl.when(has_prev)(q_tails[g].wait_recv)
        rows = turned(q_tail_in[g], qf[g, :SPAN, :])
        for h in range(heads):
            qr[g * heads + h] = rows[:, h * HEAD_DIM : (h + 1) * HEAD_DIM]

    def attend(g, first, end, opening, closing):
        span = (end - first) * SPAN

        def head(h, _):
            i = g * heads + h
            keys = kv[g, first:end, :, :HEAD_DIM].reshape(span, HEAD_DIM)
            values = kv[g, first:end, :, HEAD_DIM:].reshape(span, HEAD_DIM)
            scores = lax.dot_general(
                qr[i], keys, (((1,), (1,)), ((), ())), preferred_element_type=F32
            )
            scores = scores * SCALE + bias[:, first * SPAN : end * SPAN]
            peak = jnp.max(scores, axis=1, keepdims=True)
            if not opening:
                old = top[i]
                peak = jnp.maximum(peak, old[:, :1])
            weights = jnp.exp2(scores - peak)
            sums = jnp.sum(weights, axis=1, keepdims=True)
            product = jnp.dot(weights.astype(BF16), values, preferred_element_type=F32)
            if not opening:
                factor = jnp.exp2(old - peak)
                sums = sums + total[i] * factor
                product = product + acc[i] * factor
            if closing:
                out[g, :, pl.ds(pl.multiple_of(h * HEAD_DIM, HEAD_DIM), HEAD_DIM)] = (
                    product / sums
                ).astype(BF16)
            else:
                top[i] = jnp.broadcast_to(peak, (SPAN, HEAD_DIM))
                total[i] = jnp.broadcast_to(sums, (SPAN, HEAD_DIM))
                acc[i] = product
            return 0

        lax.fori_loop(0, heads, head, 0)

    def out_copy(g):
        return pltpu.make_async_copy(
            out.at[g], out_hbm.at[:, pl.ds(g * wide, wide)], out_sem.at[g]
        )

    for g in range(KV_HEADS):
        forward(g)
    for g in range(KV_HEADS):
        turn_q(g)
        forward_far(g)
        arrival(g, 1)
        arrival(g, 3)
        attend(g, 0, WINDOW, True, True)
        out_copy(g).start()

    for g in range(KV_HEADS):
        out_copy(g).wait()
        pl.when(has_next)(kv_tails[g].wait_send)
        pl.when(has_next)(q_tails[g].wait_send)
        pl.when(has_onward)(hop(g, 0, 2, onward).wait_send)
        pl.when(has_onward)(hop(g, 2, 4, onward).wait_send)
        hop(g, 2, 3, partner).wait_send()

        @pl.when(core == 0)
        def _():
            hop(g, 0, 1, partner).wait_send()

        @pl.when(core == 1)
        def _():
            hop(g, 2, 1, partner).wait_send()

    pl.when(has_next)(count_copy.wait_send)


def shards(query_frames, key_frames, value_frames, token_counts, segments):
    slots, qw = query_frames.shape
    heads = qw // HEAD_DIM
    wide = qw // KV_HEADS
    any_space = pl.BlockSpec(memory_space=pl.ANY)
    lanes = 2 * HEAD_DIM
    small = pltpu.VMEM((8, SPAN), F32)
    dma = pltpu.SemaphoreType.DMA
    return pl.pallas_call(
        kernel,
        out_shape=jax.ShapeDtypeStruct((SPAN, qw), BF16),
        in_specs=[any_space, any_space, any_space, pl.BlockSpec(memory_space=pltpu.SMEM), any_space],
        out_specs=any_space,
        scratch_shapes=[
            pltpu.VMEM((KV_HEADS, slots, wide), BF16),
            pltpu.VMEM((KV_HEADS, slots, lanes), BF16),
            pltpu.VMEM((segments.shape[0] // HEAD_DIM, HEAD_DIM), I32),
            small,
            small,
            small,
            small,
            pltpu.VMEM((Z, 8, SPAN), F32),
            small,
            pltpu.VMEM((X, 8, SPAN), F32),
            small,
            small,
            small,
            small,
            small,
            pltpu.VMEM((SPAN, 2 * SPAN), BF16),
            pltpu.VMEM((KV_HEADS, SPAN, lanes), BF16),
            pltpu.VMEM((KV_HEADS, SPAN, lanes), BF16),
            pltpu.VMEM((KV_HEADS, SPAN, wide), BF16),
            pltpu.VMEM((KV_HEADS, SPAN, wide), BF16),
            pltpu.VMEM((KV_HEADS, WINDOW, SPAN, lanes), BF16),
            pltpu.VMEM((heads, SPAN, HEAD_DIM), BF16),
            pltpu.VMEM((SPAN, WINDOW * SPAN), F32),
            pltpu.VMEM((KV_HEADS, SPAN, wide), BF16),
            pltpu.VMEM((heads, SPAN, HEAD_DIM), F32),
            pltpu.VMEM((heads, SPAN, HEAD_DIM), F32),
            pltpu.VMEM((heads, SPAN, HEAD_DIM), F32),
            dma((3 * KV_HEADS,)),
            dma,
            dma((KV_HEADS,)),
            dma((4,)),
            dma((4,)),
            dma((Z,)),
            dma((Z,)),
            dma((X,)),
            dma((X,)),
            dma((2 * KV_HEADS,)),
            dma((2 * KV_HEADS,)),
            dma((KV_HEADS, WINDOW)),
            dma((KV_HEADS, WINDOW)),
        ],
        compiler_params=pltpu.CompilerParams(
            collective_id=0, has_side_effects=True, vmem_limit_bytes=62 * 2**20
        ),
    )(query_frames, key_frames, value_frames, token_counts, segments.reshape(-1, HEAD_DIM))


def solution(mesh):
    share = P(("group", "seq"), None)
    return jax.shard_map(
        shards,
        mesh=mesh,
        in_specs=(share, share, share, P(("group", "seq")), P("group")),
        out_specs=share,
        check_vma=False,
    )
```

time: 193 us -> 110 us (0.57); the launches traced: 191 us -> 110 us
  Pallas kernels: 0 us -> 106 us
  blocking collectives: 45.3 us -> 0 us
  waiting for transfers between devices: 35.4 us -> 0 us
  local copies, waits for them, and re-layouts: 34.6 us -> 3.13 us
  matrix products: 26.6 us -> 0 us
  starting transfers between devices: 23.5 us -> 0 us
  other arithmetic: 22.6 us -> 0 us
    pallas_call x0 -> x1, Pallas kernels: none -> 106 us  [shards(): pl.pallas_call(kernel, out_shape=jax.ShapeDtypeStruct((SPAN, qw), BF16),...]
    unnamed x2 -> x0, blocking collectives: 45.3 us -> none
    ppermute x11 -> x0, waiting for transfers between devices: 35.4 us -> none  [passed_along(): return lax.ppermute(block, axis, route)]
    dot_general x10 -> x0, matrix products: 26.6 us -> none  [the longest x5 15.1 us: attend_block(): jnp.einsum('hgqk,khd->qhgd', weights.astype(jnp.bfloat16), value_rows.res...]
    ppermute x11 -> x0, starting transfers between devices: 23.5 us -> none  [passed_along(): return lax.ppermute(block, axis, route)]
    while x49 -> x0, local copies, waits for them, and re-layouts: 23 us -> none
    reduce_sum x6 -> x0, other arithmetic: 9.58 us -> none  [the longest x5 8.95 us: attend_block(): totals = totals * factor + jnp.sum(weights, axis=-1)]
    select_n x4 -> x0, other arithmetic: 8.08 us -> none  [the longest x1 3.47 us: shards(): queries = jnp.where(early, arrived[0], own_rows(query_frames))]
  transfers between devices with their start and end apart: 11 -> 0, of which waited for: 6 -> 0; matrix products, arithmetic and copies ran while one was open for 17% -> 0% of each run, Pallas kernels for 0% -> 0%
where the time goes in v1:
time: 110 us
  Pallas kernels  106 us (96%)
  local copies, waits for them, and re-layouts  3.13 us (3%)
    pallas_call x1, Pallas kernels, shards(): pl.pallas_call(kernel, out_shape=jax.ShapeDtypeStruct((SPAN, qw), BF16),...  106 us
    unnamed x1, local copies, waits for them, and re-layouts  3.13 us

profile of v1, /device:TPU:46, one launch (start us, length us, event | category | flops | bytes accessed | tf_op | source)
XLA Modules:
  0.0 109.8 jit_solution(17381619250225670637)
XLA Ops:
  0.7 106.0 %shard_map.55 = bf16[256,4096]{1,0:T(8,128)(2,1)} custom-call(bf16[512,4096]{1,0:T(8,128)(2,1)} %q_hbm.1, bf16[512,512]{1,0:T(8,128)(2,1)} %k_hbm.1, bf16[512,512]{1,0:T(8,128)(2,1)} %v_hbm.1, s32[1]{0:T(128)S(6)} %copy.7.count_ref, s32[256,128]{1,0:T(8,128)} %bitcast.1), custom_call_target="tpu_custom_call" | custom-call | tf_op jit(solution)/shard_map/pallas_call | solution.py:433
  106.7 3.1 %copy.8 = bf16[256,4096]{1,0:T(8,128)(2,1)} copy(bf16[256,4096]{1,0:T(8,128)(2,1)} %shard_map.55) | data formatting | bytes 4194304

commit v2 on v1

--- a/solution.py
+++ b/solution.py
@@ -13,6 +13,9 @@
 SPAN = 256
 WINDOW = 5
 X, Z = 4, 16
+HELD = 2
+RELAYED = 8
+FIRST_RELAY, SECOND_RELAY = 2 * (Z - 1) // 3, (Z - 1) // 3
 MESH = pl.DeviceIdType.MESH
 SCALE = math.log2(math.e) / math.sqrt(HEAD_DIM)
 MASKED = -1e30
@@ -53,6 +56,7 @@
     acc,
     top,
     total,
+    relay,
     load_sem,
     seg_sem,
     out_sem,
@@ -66,6 +70,8 @@
     tail_recv,
     block_send,
     block_recv,
+    relay_send,
+    relay_recv,
 ):
     n = lax.axis_size("seq")
     d = lax.axis_index("seq")
@@ -127,22 +133,53 @@
     def greet(device):
         pl.semaphore_signal(barrier, inc=1, device_id=device, device_id_type=MESH)
 
-    greet(partner)
-    greet(at(d + 2))
-    greet(at(d - 2))
-
-    @pl.when(core == 1)
-    def _():
-        greet(at(d + 1))
+    has_next, has_prev = d < n - 1, d > 0
+    has_onward, has_back = d < n - 2, d > 1
+    turning = x < X - 1
+    source = (core == 1) & turning & (z == Z - 1)
+    first_relay = (core == 1) & turning & (z == FIRST_RELAY)
+    second_relay = (core == 1) & (x > 0) & (z == SECOND_RELAY)
+    sink = (core == 0) & (x > 0) & (z == 0)
+
+    def in_column(column_x, column_z, column_core):
+        return at((column_x * Z + column_z) * 2 + column_core)
+
+    pl.when(d > 0)(lambda: greet(partner))
+    pl.when(has_back)(lambda: greet(at(d - 2)))
+    sends_on = jnp.where(has_onward, 1, 0)
+    first_chip = chip == 0
 
     @pl.when(core == 0)
     def _():
-        greet(at(d - 1))
+        pl.when(has_prev)(lambda: greet(at(d - 1)))
         lax.fori_loop(1, Z, lambda k, _: greet(z_peer(k)), None)
         lax.fori_loop(1, X, lambda k, _: greet(x_peer(k)), None)
 
+    pl.when(first_relay)(lambda: greet(in_column(x, Z - 1, 1)))
+    pl.when(second_relay)(lambda: greet(in_column(x - 1, FIRST_RELAY, 1)))
+    pl.when(sink)(lambda: greet(in_column(x, SECOND_RELAY, 1)))
+
     own_count = count_ref[0]
     count[...] = jnp.full(count.shape, own_count.astype(F32))
+
+    count_copy = remote(count, count_prev, one_send.at[0], one_recv.at[0], follower)
+    pair_copy = remote(count, count_pair, one_send.at[1], one_recv.at[1], partner)
+    before_copy = remote(before, before_in, one_send.at[2], one_recv.at[2], partner)
+
+    def zero(ref):
+        ref[...] = jnp.zeros(ref.shape, ref.dtype)
+
+    def start_if(there, copy):
+        pl.when(there)(copy.start)
+
+    @pl.when(core == 1)
+    def _():
+        also = jnp.where(source | first_relay | second_relay, 1, 0)
+        beside = jnp.where(first_chip, 0, 1)
+        pl.semaphore_wait(barrier, beside + jnp.where(has_next, 1, 0) + sends_on + also)
+        start_if(jnp.logical_not(first_chip), pair_copy)
+        start_if(has_next, count_copy)
+
     for load in loads:
         load.wait()
 
@@ -156,43 +193,83 @@
         slot = lax.broadcasted_iota(I32, (SPAN, wide), 0)
         q_tail[g] = jnp.where(slot < high, qf[g, SPAN:, :], qf[g, :SPAN, :])
 
-    select_q(0)
-    pl.semaphore_wait(barrier, jnp.where(core == 0, Z + X + 2, 4))
-
-    count_copy = remote(count, count_prev, one_send.at[0], one_recv.at[0], follower)
-    pair_copy = remote(count, count_pair, one_send.at[1], one_recv.at[1], partner)
-    before_copy = remote(before, before_in, one_send.at[2], one_recv.at[2], partner)
-    has_next, has_prev = d < n - 1, d > 0
-    has_onward, has_back = d < n - 2, d > 1
-
-    def start_if(there, copy):
-        pl.when(there)(copy.start)
-
-    start_if(has_next, count_copy)
-    start_if(core == 1, pair_copy)
-
-    kv_tails = [
-        remote(kv_tail.at[g], kv_tail_in.at[g], tail_send.at[g], tail_recv.at[g], follower)
-        for g in range(KV_HEADS)
-    ]
-    q_tails = [
-        remote(
+    def kv_tail_copy(g):
+        return remote(kv_tail.at[g], kv_tail_in.at[g], tail_send.at[g], tail_recv.at[g], follower)
+
+    def q_tail_copy(g):
+        return remote(
             q_tail.at[g],
             q_tail_in.at[g],
             tail_send.at[KV_HEADS + g],
             tail_recv.at[KV_HEADS + g],
             follower,
         )
-        for g in range(KV_HEADS)
-    ]
-    for g in range(KV_HEADS):
-        start_if(has_next, kv_tails[g])
+
+    early = (core == 1) & (z < Z // 2)
+    late = (core == 1) & (z >= Z // 2) & has_next & jnp.logical_not(source)
+    piece = relay.shape[1]
+    pieces = SPAN // piece
+
+    def tail_piece(ref, j):
+        return ref.at[HELD + j // pieces, pl.ds(lax.rem(j, pieces) * piece, piece)]
+
+    def relay_in(j, device):
+        return remote(tail_piece(q_tail, j), relay.at[j], relay_send.at[j], relay_recv.at[j], device)
+
+    def relay_on(j, device):
+        return remote(relay.at[j], relay.at[j], relay_send.at[j], relay_recv.at[j], device)
+
+    def relay_out(j, device):
+        arrived = tail_recv.at[KV_HEADS + HELD + j // pieces]
+        return remote(relay.at[j], tail_piece(q_tail_in, j), relay_send.at[j], arrived, device)
+
+    select_q(0)
+
+    @pl.when(core == 1)
+    def _():
+        for g in range(KV_HEADS):
+            start_if(has_next, kv_tail_copy(g))
+
     select_q(1)
-    start_if(has_next, q_tails[0])
+    start_if((core == 1) & has_next, q_tail_copy(0))
     select_q(2)
-    start_if(has_next, q_tails[1])
+    start_if((core == 1) & has_next, q_tail_copy(1))
     select_q(3)
-    pl.when(has_prev)(count_copy.wait_recv)
+
+    @pl.when(early)
+    def _():
+        for g in range(HELD, KV_HEADS):
+            q_tail_copy(g).start()
+
+    @pl.when(source)
+    def _():
+        to = in_column(x, FIRST_RELAY, 1)
+        lax.fori_loop(0, RELAYED, lambda j, _: relay_in(j, to).start(), None)
+
+    @pl.when(first_relay)
+    def _():
+        to = in_column(x + 1, SECOND_RELAY, 1)
+
+        def pass_on(j, _):
+            relay_on(j, to).wait_recv()
+            relay_on(j, to).start()
+
+        lax.fori_loop(0, RELAYED, pass_on, None)
+
+    @pl.when(second_relay)
+    def _():
+        to = in_column(x, 0, 0)
+
+        def pass_out(j, _):
+            relay_on(j, to).wait_recv()
+            relay_out(j, to).start()
+
+        lax.fori_loop(0, RELAYED, pass_out, None)
+
+    @pl.when(core == 0)
+    def _():
+        pl.semaphore_wait(barrier, Z + X - 1 + sends_on)
+        count_copy.start()
 
     @pl.when(d == 0)
     def _():
@@ -207,7 +284,11 @@
 
     @pl.when(core == 0)
     def _():
-        pair_copy.wait_recv()
+        @pl.when(first_chip)
+        def _():
+            count_pair[...] = jnp.zeros(count_pair.shape, F32)
+
+        pl.when(jnp.logical_not(first_chip))(pair_copy.wait_recv)
         pair_sum[...] = count[...] + count_pair[...]
         column[pl.ds(z, 1)] = pair_sum[...][None]
 
@@ -220,8 +301,20 @@
                 pair_sum, column.at[other], z_send.at[k], z_recv.at[other], z_peer(k)
             )
 
-        lax.fori_loop(1, Z, lambda k, _: z_copy(k).start(), None)
-        lax.fori_loop(1, Z, lambda k, _: z_from(k).wait_recv(), None)
+        pl.when((x == 0) & (z > 0))(lambda: zero(column.at[0]))
+
+        @pl.when(jnp.logical_not(first_chip))
+        def _():
+            lax.fori_loop(1, Z, lambda k, _: z_copy(k).start(), None)
+
+        for g in range(KV_HEADS):
+            kv_tail_copy(g).start()
+            q_tail_copy(g).start()
+
+        def z_arrival(k, _):
+            pl.when((x > 0) | (lax.rem(z + k, Z) > 0))(z_from(k).wait_recv)
+
+        lax.fori_loop(1, Z, z_arrival, None)
         z_place = lax.broadcasted_iota(I32, column.shape, 0)
         x_place = lax.broadcasted_iota(I32, columns.shape, 0)
         base_copy = remote(base, base_in, one_send.at[3], one_recv.at[3], z_peer(Z - 1))
@@ -234,6 +327,8 @@
             return remote(
                 column_sum, columns.at[other], x_send.at[k], x_recv.at[other], x_peer(k)
             )
+
+        pl.when(has_prev)(count_copy.wait_recv)
 
         @pl.when(z > 0)
         def _():
@@ -243,18 +338,24 @@
                 x_copy(k).start()
             for k in range(1, X):
                 x_from(k).wait_recv()
-            base[...] = jnp.sum(jnp.where(x_place < x, columns[...], 0.0), axis=0)
+            base[...] = jnp.sum(jnp.where(x_place > x, columns[...], 0.0), axis=0)
             pl.when(z == 1)(base_copy.start)
-            before[...] = base[...] + jnp.sum(jnp.where(z_place < z, column[...], 0.0), axis=0)
+            later = jnp.sum(jnp.where(z_place >= z, column[...], 0.0), axis=0)
+            before[...] = float(n * SPAN) - (base[...] + later)
 
         @pl.when(z == 0)
         def _():
             base_copy.wait_recv()
-            before[...] = base_in[...]
+            later = base_in[...] + jnp.sum(column[...], axis=0)
+            before[...] = jnp.where(first_chip, 0.0, float(n * SPAN) - later)
 
         before_copy.start()
         lead[...] = before[...] - (d * SPAN).astype(F32)
-        lax.fori_loop(1, Z, lambda k, _: z_copy(k).wait_send(), None)
+
+        @pl.when(jnp.logical_not(first_chip))
+        def _():
+            lax.fori_loop(1, Z, lambda k, _: z_copy(k).wait_send(), None)
+
 
         @pl.when(z > 0)
         def _():
@@ -266,9 +367,10 @@
 
     @pl.when(core == 1)
     def _():
+        count_copy.wait_recv()
         before_copy.wait_recv()
         lead[...] = before_in[...] + count_prev[...] - (d * SPAN).astype(F32)
-        pair_copy.wait_send()
+        pl.when(jnp.logical_not(first_chip))(pair_copy.wait_send)
 
     lead_in = lead[0:1, :].astype(I32)
     lead_before = (lead[0:1, :] - count_prev[0:1, :]).astype(I32)
@@ -297,7 +399,7 @@
         hop(g, target, target, partner).wait_recv()
 
     for g in range(KV_HEADS):
-        pl.when(has_prev)(kv_tails[g].wait_recv)
+        pl.when(has_prev)(kv_tail_copy(g).wait_recv)
         kv[g, 0] = turned(kv_tail_in[g], kvf[g, :SPAN, :])
 
     seg_load.wait()
@@ -341,15 +443,16 @@
         def _():
             hop(g, 4, 3, partner).start()
 
-    send_own(0)
-    send_own(1)
-    start_if(has_next, q_tails[2])
-    send_own(2)
-    send_own(3)
-    start_if(has_next, q_tails[3])
+    for g in range(KV_HEADS):
+        send_own(g)
+
+    @pl.when(late)
+    def _():
+        for g in range(HELD, KV_HEADS):
+            q_tail_copy(g).start()
 
     def turn_q(g):
-        pl.when(has_prev)(q_tails[g].wait_recv)
+        pl.when(has_prev)(q_tail_copy(g).wait_recv)
         rows = turned(q_tail_in[g], qf[g, :SPAN, :])
         for h in range(heads):
             qr[g * heads + h] = rows[:, h * HEAD_DIM : (h + 1) * HEAD_DIM]
@@ -386,27 +489,45 @@
                 acc[i] = product
             return 0
 
-        lax.fori_loop(0, heads, head, 0)
+        lax.fori_loop(0, heads, head, 0, unroll=4)
 
     def out_copy(g):
         return pltpu.make_async_copy(
             out.at[g], out_hbm.at[:, pl.ds(g * wide, wide)], out_sem.at[g]
         )
 
-    for g in range(KV_HEADS):
+    def own_step(g, _):
+        turn_q(g)
+        attend(g, 0, 1, True, False)
+
+    def near_step(g, _):
+        arrival(g, 1)
+        attend(g, 1, 3, False, False)
+        forward(g + HELD)
+
+    def held_step(g, _):
+        turn_q(g)
+        arrival(g, 1)
+        attend(g, 0, 3, True, False)
+
+    def far_step(g, _):
+        forward_far(g)
+        arrival(g, 3)
+        attend(g, 3, WINDOW, False, True)
+        out_copy(g).start()
+
+    lax.fori_loop(0, HELD, own_step, None)
+    for g in range(HELD):
         forward(g)
-    for g in range(KV_HEADS):
-        turn_q(g)
-        forward_far(g)
-        arrival(g, 1)
-        arrival(g, 3)
-        attend(g, 0, WINDOW, True, True)
-        out_copy(g).start()
+    lax.fori_loop(0, HELD, near_step, None)
+    lax.fori_loop(HELD, KV_HEADS, held_step, None)
+    lax.fori_loop(0, KV_HEADS, far_step, None)
 
     for g in range(KV_HEADS):
         out_copy(g).wait()
-        pl.when(has_next)(kv_tails[g].wait_send)
-        pl.when(has_next)(q_tails[g].wait_send)
+        pl.when(has_next)(kv_tail_copy(g).wait_send)
+        straight = has_next if g < HELD else has_next & jnp.logical_not(source)
+        pl.when(straight)(q_tail_copy(g).wait_send)
         pl.when(has_onward)(hop(g, 0, 2, onward).wait_send)
         pl.when(has_onward)(hop(g, 2, 4, onward).wait_send)
         hop(g, 2, 3, partner).wait_send()
@@ -420,6 +541,10 @@
             hop(g, 2, 1, partner).wait_send()
 
     pl.when(has_next)(count_copy.wait_send)
+
+    @pl.when(source | first_relay | second_relay)
+    def _():
+        lax.fori_loop(0, RELAYED, lambda j, _: relay_on(j, partner).wait_send(), None)
 
 
 def shards(query_frames, key_frames, value_frames, token_counts, segments):
@@ -463,6 +588,7 @@
             pltpu.VMEM((heads, SPAN, HEAD_DIM), F32),
             pltpu.VMEM((heads, SPAN, HEAD_DIM), F32),
             pltpu.VMEM((heads, SPAN, HEAD_DIM), F32),
+            pltpu.VMEM((RELAYED, (KV_HEADS - HELD) * SPAN // RELAYED, wide), BF16),
             dma((3 * KV_HEADS,)),
             dma,
             dma((KV_HEADS,)),
@@ -476,6 +602,8 @@
             dma((2 * KV_HEADS,)),
             dma((KV_HEADS, WINDOW)),
             dma((KV_HEADS, WINDOW)),
+            dma((RELAYED,)),
+            dma((RELAYED,)),
         ],
         compiler_params=pltpu.CompilerParams(
             collective_id=0, has_side_effects=True, vmem_limit_bytes=62 * 2**20

time: 110 us -> 90.3 us (0.82)
  Pallas kernels: 106 us -> 86.4 us
    pallas_call x1, Pallas kernels: 106 us -> 86.4 us  [shards(): pl.pallas_call(kernel, out_shape=jax.ShapeDtypeStruct((SPAN, qw), BF16),...]
where the time goes in v2:
time: 90.3 us; the launch traced here: 90.2 us
  Pallas kernels  86.4 us (96%)
  local copies, waits for them, and re-layouts  3.13 us (3%)
    pallas_call x1, Pallas kernels, shards(): pl.pallas_call(kernel, out_shape=jax.ShapeDtypeStruct((SPAN, qw), BF16),...  86.4 us
    unnamed x1, local copies, waits for them, and re-layouts  3.13 us

profile of v2, /device:TPU:46, one launch (start us, length us, event | category | flops | bytes accessed | tf_op | source)
XLA Modules:
  0.0 90.2 jit_solution(576142046263254024)
XLA Ops:
  0.7 86.4 %shard_map.55 = bf16[256,4096]{1,0:T(8,128)(2,1)} custom-call(bf16[512,4096]{1,0:T(8,128)(2,1)} %q_hbm.1, bf16[512,512]{1,0:T(8,128)(2,1)} %k_hbm.1, bf16[512,512]{1,0:T(8,128)(2,1)} %v_hbm.1, s32[1]{0:T(128)S(6)} %copy.7.count_ref, s32[256,128]{1,0:T(8,128)} %bitcast.1), custom_call_target="tpu_custom_call" | custom-call | tf_op jit(solution)/shard_map/pallas_call | solution.py:558
  87.1 3.1 %copy.8 = bf16[256,4096]{1,0:T(8,128)(2,1)} copy(bf16[256,4096]{1,0:T(8,128)(2,1)} %shard_map.55) | data formatting | bytes 4194304

commit v3 on v2

--- a/solution.py
+++ b/solution.py
@@ -99,12 +99,6 @@
             device_id_type=MESH,
         )
 
-    def z_peer(k):
-        return at(x * (2 * Z) + 2 * lax.rem(z + k, Z) + core)
-
-    def x_peer(k):
-        return at(lax.rem(x + k, X) * (2 * Z) + 2 * z + core)
-
     loads = []
     for g in range(KV_HEADS):
         columns_of = pl.ds(g * HEAD_DIM, HEAD_DIM)
@@ -133,6 +127,9 @@
     def greet(device):
         pl.semaphore_signal(barrier, inc=1, device_id=device, device_id_type=MESH)
 
+    column[...] = jnp.zeros(column.shape, F32)
+    columns[...] = jnp.zeros(columns.shape, F32)
+
     has_next, has_prev = d < n - 1, d > 0
     has_onward, has_back = d < n - 2, d > 1
     turning = x < X - 1
@@ -148,12 +145,22 @@
     pl.when(has_back)(lambda: greet(at(d - 2)))
     sends_on = jnp.where(has_onward, 1, 0)
     first_chip = chip == 0
+    below = (z == 0) & (x > 0)
 
     @pl.when(core == 0)
     def _():
         pl.when(has_prev)(lambda: greet(at(d - 1)))
-        lax.fori_loop(1, Z, lambda k, _: greet(z_peer(k)), None)
-        lax.fori_loop(1, X, lambda k, _: greet(x_peer(k)), None)
+
+        @pl.when(z > 0)
+        def _():
+            lax.fori_loop(z + 1, Z, lambda k, _: greet(in_column(x, k, 0)), None)
+
+        pl.when((z > 1) | below)(lambda: greet(in_column(x, 1, 0)))
+
+        @pl.when(z == 1)
+        def _():
+            pl.when(x > 0)(lambda: greet(in_column(x, 0, 0)))
+            lax.fori_loop(x + 1, X, lambda k, _: greet(in_column(k, 1, 0)), None)
 
     pl.when(first_relay)(lambda: greet(in_column(x, Z - 1, 1)))
     pl.when(second_relay)(lambda: greet(in_column(x - 1, FIRST_RELAY, 1)))
@@ -268,7 +275,8 @@
 
     @pl.when(core == 0)
     def _():
-        pl.semaphore_wait(barrier, Z + X - 1 + sends_on)
+        summing = jnp.where(z == 1, Z - 2 + jnp.minimum(x, 1) + x, jnp.maximum(z - 1, 0))
+        pl.semaphore_wait(barrier, 1 + sends_on + summing + jnp.where(below, 1, 0))
         count_copy.start()
 
     @pl.when(d == 0)
@@ -292,77 +300,83 @@
         pair_sum[...] = count[...] + count_pair[...]
         column[pl.ds(z, 1)] = pair_sum[...][None]
 
-        def z_copy(k):
-            return remote(pair_sum, column.at[z], z_send.at[k], z_recv.at[z], z_peer(k))
-
-        def z_from(k):
-            other = lax.rem(z + k, Z)
+        def pair_to(k):
             return remote(
-                pair_sum, column.at[other], z_send.at[k], z_recv.at[other], z_peer(k)
+                pair_sum, column.at[z], z_send.at[k], z_recv.at[z], in_column(x, k, 0)
             )
 
-        pl.when((x == 0) & (z > 0))(lambda: zero(column.at[0]))
-
-        @pl.when(jnp.logical_not(first_chip))
-        def _():
-            lax.fori_loop(1, Z, lambda k, _: z_copy(k).start(), None)
-
+        def pair_from(k):
+            return remote(
+                pair_sum, column.at[k], z_send.at[k], z_recv.at[k], in_column(x, k, 0)
+            )
+
+        def column_to(k):
+            return remote(
+                column_sum, columns.at[x], x_send.at[k], x_recv.at[x], in_column(k, 1, 0)
+            )
+
+        def column_from(k):
+            return remote(
+                column_sum, columns.at[k], x_send.at[k], x_recv.at[k], in_column(k, 1, 0)
+            )
+
+        def base_to(k):
+            return remote(base, base_in, z_send.at[k], one_recv.at[3], in_column(x, k, 0))
+
+        base_below = remote(base_in, base_in, z_send.at[0], one_recv.at[3], in_column(x, 0, 0))
+
+        lax.fori_loop(1, z, lambda k, _: pair_to(k).start(), None)
+        pl.when(below)(lambda: pair_to(1).start())
         for g in range(KV_HEADS):
             kv_tail_copy(g).start()
             q_tail_copy(g).start()
 
-        def z_arrival(k, _):
-            pl.when((x > 0) | (lax.rem(z + k, Z) > 0))(z_from(k).wait_recv)
-
-        lax.fori_loop(1, Z, z_arrival, None)
+        @pl.when(z > 0)
+        def _():
+            lax.fori_loop(z + 1, Z, lambda k, _: pair_from(k).wait_recv(), None)
+
         z_place = lax.broadcasted_iota(I32, column.shape, 0)
         x_place = lax.broadcasted_iota(I32, columns.shape, 0)
-        base_copy = remote(base, base_in, one_send.at[3], one_recv.at[3], z_peer(Z - 1))
-
-        def x_copy(k):
-            return remote(column_sum, columns.at[x], x_send.at[k], x_recv.at[x], x_peer(k))
-
-        def x_from(k):
-            other = lax.rem(x + k, X)
-            return remote(
-                column_sum, columns.at[other], x_send.at[k], x_recv.at[other], x_peer(k)
-            )
-
+        rows = float(n * SPAN)
+
+        @pl.when(z == 1)
+        def _():
+            pl.when(x > 0)(lambda: pair_from(0).wait_recv())
+            column_sum[...] = jnp.sum(column[...], axis=0)
+            lax.fori_loop(0, x, lambda k, _: column_to(k).start(), None)
+            lax.fori_loop(x + 1, X, lambda k, _: column_from(k).wait_recv(), None)
+            base[...] = jnp.sum(jnp.where(x_place > x, columns[...], 0.0), axis=0)
+            base_in[...] = base[...] + column_sum[...]
+            lax.fori_loop(2, Z, lambda k, _: base_to(k).start(), None)
+            pl.when(x > 0)(base_below.start)
+            later = jnp.sum(jnp.where(z_place >= z, column[...], 0.0), axis=0)
+            before[...] = rows - (base[...] + later)
+
+        @pl.when(z > 1)
+        def _():
+            base_to(z).wait_recv()
+            later = jnp.sum(jnp.where(z_place >= z, column[...], 0.0), axis=0)
+            before[...] = rows - (base_in[...] + later)
+
+        @pl.when(below)
+        def _():
+            base_below.wait_recv()
+            before[...] = rows - base_in[...]
+
+        pl.when(first_chip)(lambda: zero(before))
         pl.when(has_prev)(count_copy.wait_recv)
-
-        @pl.when(z > 0)
-        def _():
-            column_sum[...] = jnp.sum(column[...], axis=0)
-            columns[pl.ds(x, 1)] = column_sum[...][None]
-            for k in range(1, X):
-                x_copy(k).start()
-            for k in range(1, X):
-                x_from(k).wait_recv()
-            base[...] = jnp.sum(jnp.where(x_place > x, columns[...], 0.0), axis=0)
-            pl.when(z == 1)(base_copy.start)
-            later = jnp.sum(jnp.where(z_place >= z, column[...], 0.0), axis=0)
-            before[...] = float(n * SPAN) - (base[...] + later)
-
-        @pl.when(z == 0)
-        def _():
-            base_copy.wait_recv()
-            later = base_in[...] + jnp.sum(column[...], axis=0)
-            before[...] = jnp.where(first_chip, 0.0, float(n * SPAN) - later)
-
         before_copy.start()
         lead[...] = before[...] - (d * SPAN).astype(F32)
 
-        @pl.when(jnp.logical_not(first_chip))
-        def _():
-            lax.fori_loop(1, Z, lambda k, _: z_copy(k).wait_send(), None)
-
-
-        @pl.when(z > 0)
-        def _():
-            for k in range(1, X):
-                x_copy(k).wait_send()
-
-        pl.when(z == 1)(base_copy.wait_send)
+        lax.fori_loop(1, z, lambda k, _: pair_to(k).wait_send(), None)
+        pl.when(below)(lambda: pair_to(1).wait_send())
+
+        @pl.when(z == 1)
+        def _():
+            lax.fori_loop(0, x, lambda k, _: column_to(k).wait_send(), None)
+            lax.fori_loop(2, Z, lambda k, _: base_to(k).wait_send(), None)
+            pl.when(x > 0)(base_below.wait_send)
+
         before_copy.wait_send()
 
     @pl.when(core == 1)
@@ -489,7 +503,7 @@
                 acc[i] = product
             return 0
 
-        lax.fori_loop(0, heads, head, 0, unroll=4)
+        lax.fori_loop(0, heads, head, 0, unroll=8)
 
     def out_copy(g):
         return pltpu.make_async_copy(
@@ -503,12 +517,7 @@
     def near_step(g, _):
         arrival(g, 1)
         attend(g, 1, 3, False, False)
-        forward(g + HELD)
-
-    def held_step(g, _):
-        turn_q(g)
-        arrival(g, 1)
-        attend(g, 0, 3, True, False)
+        pl.when(z < Z - 1)(lambda: forward(g + HELD))
 
     def far_step(g, _):
         forward_far(g)
@@ -516,12 +525,29 @@
         attend(g, 3, WINDOW, False, True)
         out_copy(g).start()
 
+    def whole_step(g, _):
+        turn_q(g)
+        forward_far(g)
+        arrival(g, 1)
+        arrival(g, 3)
+        attend(g, 0, WINDOW, True, True)
+        out_copy(g).start()
+
+    @pl.when(z == Z - 1)
+    def _():
+        for g in range(KV_HEADS):
+            forward(g)
+
     lax.fori_loop(0, HELD, own_step, None)
-    for g in range(HELD):
-        forward(g)
+
+    @pl.when(z < Z - 1)
+    def _():
+        for g in range(HELD):
+            forward(g)
+
     lax.fori_loop(0, HELD, near_step, None)
-    lax.fori_loop(HELD, KV_HEADS, held_step, None)
-    lax.fori_loop(0, KV_HEADS, far_step, None)
+    lax.fori_loop(0, HELD, far_step, None)
+    lax.fori_loop(HELD, KV_HEADS, whole_step, None)
 
     for g in range(KV_HEADS):
         out_copy(g).wait()

time: 90.3 us -> 86.4 us (0.957)
  Pallas kernels: 86.4 us -> 82.4 us
    pallas_call x1, Pallas kernels: 86.4 us -> 82.4 us  [shards(): pl.pallas_call(kernel, out_shape=jax.ShapeDtypeStruct((SPAN, qw), BF16),...]
where the time goes in v3:
time: 86.4 us; the launch traced here: 86.2 us
  Pallas kernels  82.4 us (95%)
  local copies, waits for them, and re-layouts  3.13 us (4%)
    pallas_call x1, Pallas kernels, shards(): pl.pallas_call(kernel, out_shape=jax.ShapeDtypeStruct((SPAN, qw), BF16),...  82.4 us
    unnamed x1, local copies, waits for them, and re-layouts  3.13 us

profile of v3, /device:TPU:46, one launch (start us, length us, event | category | flops | bytes accessed | tf_op | source)
XLA Modules:
  0.0 86.2 jit_solution(9596087075194656456)
XLA Ops:
  0.7 82.4 %shard_map.55 = bf16[256,4096]{1,0:T(8,128)(2,1)} custom-call(bf16[512,4096]{1,0:T(8,128)(2,1)} %q_hbm.1, bf16[512,512]{1,0:T(8,128)(2,1)} %k_hbm.1, bf16[512,512]{1,0:T(8,128)(2,1)} %v_hbm.1, s32[1]{0:T(128)S(6)} %copy.7.count_ref, s32[256,128]{1,0:T(8,128)} %bitcast.1), custom_call_target="tpu_custom_call" | custom-call | tf_op jit(solution)/shard_map/pallas_call | solution.py:584
  83.1 3.1 %copy.8 = bf16[256,4096]{1,0:T(8,128)(2,1)} copy(bf16[256,4096]{1,0:T(8,128)(2,1)} %shard_map.55) | data formatting | bytes 4194304

commit v4 on v3

--- a/solution.py
+++ b/solution.py
@@ -14,7 +14,7 @@
 WINDOW = 5
 X, Z = 4, 16
 HELD = 2
-RELAYED = 8
+RELAYED = 16
 FIRST_RELAY, SECOND_RELAY = 2 * (Z - 1) // 3, (Z - 1) // 3
 MESH = pl.DeviceIdType.MESH
 SCALE = math.log2(math.e) / math.sqrt(HEAD_DIM)
@@ -527,7 +527,6 @@
 
     def whole_step(g, _):
         turn_q(g)
-        forward_far(g)
         arrival(g, 1)
         arrival(g, 3)
         attend(g, 0, WINDOW, True, True)
@@ -547,6 +546,8 @@
 
     lax.fori_loop(0, HELD, near_step, None)
     lax.fori_loop(0, HELD, far_step, None)
+    for g in range(HELD, KV_HEADS):
+        forward_far(g)
     lax.fori_loop(HELD, KV_HEADS, whole_step, None)
 
     for g in range(KV_HEADS):

time: 86.4 us -> 86.7 us (level)
  no operation moved by 1% of the time
where the time goes in v4:
time: 86.7 us; the launch traced here: 86.5 us
  Pallas kernels  82.7 us (95%)
  local copies, waits for them, and re-layouts  3.13 us (4%)
    pallas_call x1, Pallas kernels, shards(): pl.pallas_call(kernel, out_shape=jax.ShapeDtypeStruct((SPAN, qw), BF16),...  82.7 us
    unnamed x1, local copies, waits for them, and re-layouts  3.13 us

profile of v4, /device:TPU:46, one launch (start us, length us, event | category | flops | bytes accessed | tf_op | source)
XLA Modules:
  0.0 86.5 jit_solution(4520724042773213888)
XLA Ops:
  0.7 82.7 %shard_map.55 = bf16[256,4096]{1,0:T(8,128)(2,1)} custom-call(bf16[512,4096]{1,0:T(8,128)(2,1)} %q_hbm.1, bf16[512,512]{1,0:T(8,128)(2,1)} %k_hbm.1, bf16[512,512]{1,0:T(8,128)(2,1)} %v_hbm.1, s32[1]{0:T(128)S(6)} %copy.7.count_ref, s32[256,128]{1,0:T(8,128)} %bitcast.1), custom_call_target="tpu_custom_call" | custom-call | tf_op jit(solution)/shard_map/pallas_call | solution.py:585
  83.4 3.1 %copy.8 = bf16[256,4096]{1,0:T(8,128)(2,1)} copy(bf16[256,4096]{1,0:T(8,128)(2,1)} %shard_map.55) | data formatting | bytes 4194304
